TPU v7x, 32 devices: a whole 2x2x4 slice. The times are simulated.
32 devices in a mesh: member: 2 (over x), gx: 8 (over z, y), gy: 2 (over core).
Axes of the slice: x: 2, y: 2, z: 4, core: 2. Of those that a mesh axis runs over, the one named last changes fastest.
Arguments:
- conc: float32 [66, 4, 64, 256], P(None, None, ('member', 'gx'), 'gy'), parts along dimension 2, may hold values from 0.001 to 30
- winds: float32 [2, 4, 64, 256], P(None, None, ('member', 'gx'), 'gy'), parts along dimension 2, may hold values from -0.9 to 0.9
- diffusivity: float32 [3, 64, 256], P(None, ('member', 'gx'), 'gy'), parts along dimension 1, may hold values from 0.1 to 10
- emission: float32 [66, 64, 256], P(None, ('member', 'gx'), 'gy'), parts along dimension 1, may hold values from 0.1 to 1
- photo_rate: float32 [66], replicated, may hold values from 0.05 to 1
Outputs:
- conc_next: float32 [66, 4, 64, 256], P(None, None, ('member', 'gx'), 'gy'), parts along dimension 2
There are 2 independent parts, one for each index of `member`. A program takes and returns all parts, laid end to end along the dimension named above; an argument that names none is the same for every part. Nothing has to cross between parts.
All inputs are finite; a program needn't handle non-finite values.
Results may differ from a plain program's by a relative error of at most 0.00002.
Values sent between devices are 32-bit elements; how exact they have to be, the bound alone decides.
A program may use at most 64 MiB of HBM per device.

v0:
```python
import functools

import jax
import jax.numpy as jnp
from jax import lax
from jax.experimental import pallas as pl
from jax.experimental.pallas import tpu as pltpu
from jax.sharding import PartitionSpec as P

BETAS = (1.0 / 3.0, 0.5, 1.0)
SUB = 8
LANES = 128
PAD = 3
CHUNKS = 3


def stencil_weights(km, kp):
    def face(k):
        k = k / 60.0
        a = jnp.abs(k)
        return (
            k + a,
            -8.0 * k - 5.0 * a,
            37.0 * k + 10.0 * a,
            37.0 * k - 10.0 * a,
            -8.0 * k + 5.0 * a,
            k - a,
        )

    m, p = face(km), face(kp)
    return [-m[0]] + [p[j] - m[j + 1] for j in range(5)] + [p[5]]


def kernel(dims, conc_hbm, wind_hbm, diff_hbm, emis_hbm, rate_ref, out_ref,
           conc_ref, wind_ref, diff_ref, emis_ref,
           send, state0, state_a, state_b, result, back, wsend, wrecv, cbuf, wx, wy,
           stat, stats, prate, coef,
           load_sem, in_send, in_recv, w_send, w_recv, h_send, h_recv,
           out_send, out_recv, s_send, s_recv):
    spec, lev, rows, halves, gx_n, span, tiles, chunks = dims
    n = gx_n * halves
    width = tiles // chunks
    deep = span * rows
    crews = gx_n // span
    my_gx, my_gy = lax.axis_index("gx"), lax.axis_index("gy")
    me = my_gx * halves + my_gy
    crew, seat = my_gx // span, my_gx % span
    my_lev = seat * halves + my_gy
    has_down, has_up = crew > 0, crew < crews - 1

    def where_is(dev):
        return {"gx": dev // halves, "gy": dev % halves}

    barrier = pltpu.get_barrier_semaphore()

    def greet(k, carry):
        pl.semaphore_signal(barrier, inc=1, device_id=where_is((me + k) % n),
                            device_id_type=pl.DeviceIdType.MESH)
        return carry

    lax.fori_loop(1, n, greet, 0)
    loads = [pltpu.make_async_copy(src, dst, load_sem.at[i]) for i, (src, dst) in enumerate(
        ((wind_hbm, wind_ref), (conc_hbm, conc_ref), (diff_hbm, diff_ref), (emis_hbm, emis_ref)))]
    for load in loads:
        load.start()

    stride = lev * rows
    loads[0].wait()
    for lv in range(lev):
        wsend[lv, 0:rows, :] = wind_ref[pl.ds(lv * rows, rows), :]
        wsend[lv, rows:2 * rows, :] = wind_ref[pl.ds((lev + lv) * rows, rows), :]
    loads[1].wait()
    for t in range(tiles):
        have = max(0, min(SUB, spec - t * SUB))
        for lv in range(lev):
            for r in range(rows):
                if have < SUB:
                    send[lv, t, r, :, :] = jnp.zeros((SUB, LANES), jnp.float32)
                if have > 0:
                    send[lv, t, r, 0:have, :] = conc_ref[
                        pl.ds(t * SUB * stride + lv * rows + r, have, stride=stride), :]

    pl.semaphore_wait(barrier, n - 1)

    def remote(src, dst, dev, s_sem, r_sem):
        return pltpu.make_async_remote_copy(
            src_ref=src, dst_ref=dst, send_sem=s_sem, recv_sem=r_sem,
            device_id=where_is(dev), device_id_type=pl.DeviceIdType.MESH)

    def deliver(src, dst, dev, s_sem, r_sem):
        @pl.when(dev == me)
        def _():
            pltpu.make_async_copy(src, dst, r_sem).start()

        @pl.when(dev != me)
        def _():
            remote(src, dst, dev, s_sem, r_sem).start()

    def sent(src, s_sem):
        pltpu.make_async_copy(src, src, s_sem).wait()

    def landed(dst, r_sem):
        pltpu.make_async_copy(dst, dst, r_sem).wait()

    def mate(lv):
        return (crew * span + lv // halves) * halves + lv % halves

    def tile_range(c):
        return pl.ds(c * width, width)

    sides = ((0, None, None), (1, has_up & (seat == span - 1), 0),
             (-1, has_down & (seat == 0), span + 1))

    def for_winds(act):
        for o, (shift, cond, slot) in enumerate(sides):
            at = seat + 1 if slot is None else slot
            for lv in range(lev):
                dev = mate(lv) + shift * span * halves
                if cond is None:
                    act(o, lv, dev, at)
                else:
                    pl.when(cond)(functools.partial(act, o, lv, dev, at))

    for_winds(lambda o, lv, dev, at: deliver(
        wsend.at[lv], wrecv.at[at * halves + my_gy], dev, w_send.at[o, lv],
        w_recv.at[at * halves + my_gy]))
    for c in range(chunks):
        for lv in range(lev):
            deliver(send.at[lv, tile_range(c)],
                    state0.at[tile_range(c), my_gy, pl.ds(PAD + seat * rows, rows)],
                    mate(lv), in_send.at[lv, c], in_recv.at[my_lev, c])

    lane = lax.broadcasted_iota(jnp.int32, (SUB, LANES), 1)
    states = (state0, state_a, state_b)
    blank = jnp.zeros((PAD, SUB, LANES), jnp.float32)

    @pl.when(crew == 0)
    def _():
        for buf in states:
            for t in range(tiles):
                for h in range(halves):
                    buf[t, h, 0:PAD] = blank

    @pl.when(crew == crews - 1)
    def _():
        for buf in states:
            for t in range(tiles):
                for h in range(halves):
                    buf[t, h, PAD + deep:2 * PAD + deep] = blank

    for h in range(halves):
        for c in range(2):
            cbuf[c, h, 0:SUB, :] = jnp.zeros((SUB, LANES), jnp.float32)
            cbuf[c, h, SUB + deep:2 * SUB + deep, :] = jnp.zeros((SUB, LANES), jnp.float32)

    def wind_in(slot):
        for h in range(halves):
            landed(wrecv.at[slot * halves + h], w_recv.at[slot * halves + h])
            for c in range(2):
                base = SUB + (slot - 1) * rows
                cbuf[c, h, base:base + rows, :] = wrecv[
                    slot * halves + h, c * rows:(c + 1) * rows, :]

    for slot in range(1, span + 1):
        wind_in(slot)
    pl.when(has_down)(lambda: wind_in(0))
    pl.when(has_up)(lambda: wind_in(span + 1))
    for x0 in range(0, deep, SUB):
        for h in range(halves):
            here = cbuf[0, h, SUB + x0:SUB + x0 + SUB, :]
            left = cbuf[0, h, SUB + x0 - 1:SUB + x0 - 1 + SUB, :]
            right = cbuf[0, h, SUB + x0 + 1:SUB + x0 + 1 + SUB, :]
            for j, w in enumerate(stencil_weights(0.5 * (left + here), 0.5 * (here + right))):
                wx[j, h, x0:x0 + SUB, :] = w
        cy = [cbuf[1, h, SUB + x0:SUB + x0 + SUB, :] for h in range(halves)]
        zer = jnp.zeros((SUB, LANES), jnp.float32)
        for h in range(halves):
            nxt = pltpu.roll(cy[h + 1], LANES - 1, 1) if h + 1 < halves else zer
            prv = pltpu.roll(cy[h - 1], 1, 1) if h > 0 else zer
            up = jnp.where(lane < LANES - 1, pltpu.roll(cy[h], LANES - 1, 1), nxt)
            down = jnp.where(lane >= 1, pltpu.roll(cy[h], 1, 1), prv)
            ws = stencil_weights(0.5 * (down + cy[h]), 0.5 * (cy[h] + up))
            for j, w in enumerate(ws):
                d = j - 3
                if d > 0 and h == halves - 1:
                    w = jnp.where(lane < LANES - d, w, 0.0)
                if d < 0 and h == 0:
                    w = jnp.where(lane >= -d, w, 0.0)
                wy[j, h, x0:x0 + SUB, :] = w

    def halo(s, c, d):
        buf, own = states[s], tile_range(c)
        first, land = (deep, 0) if d == 0 else (PAD, PAD + deep)
        return remote(
            buf.at[own, :, pl.ds(first, PAD)], buf.at[own, :, pl.ds(land, PAD)],
            me + (span * halves if d == 0 else -span * halves),
            h_send.at[s, c, d], h_recv.at[s, c, d])

    def start_halo(s, c):
        pl.when(has_up)(lambda: halo(s, c, 0).start())
        pl.when(has_down)(lambda: halo(s, c, 1).start())

    def wait_halo(s, c):
        own = tile_range(c)
        pl.when(has_down)(lambda: landed(states[s].at[own, :, pl.ds(0, PAD)], h_recv.at[s, c, 0]))
        pl.when(has_up)(lambda: landed(
            states[s].at[own, :, pl.ds(PAD + deep, PAD)], h_recv.at[s, c, 1]))

    for c in range(chunks):
        for lv in range(lev):
            landed(state0.at[tile_range(c), lv % halves, pl.ds(PAD + (lv // halves) * rows, rows)],
                   in_recv.at[lv, c])
        start_halo(0, c)

    def stage(c, src, dst, off, beta, x, sums):
        wxs = [[wx[j, h, pl.ds(x, 1), :] * beta for j in range(7)] for h in range(halves)]
        wys = [[wy[j, h, pl.ds(x, 1), :] * beta for j in range(7)] for h in range(halves)]
        out = []
        for i in range(width):
            t = c * width + i
            partial, new = [], []
            for h in range(halves):
                acc = wxs[h][0] * src[t, h, x]
                for j in range(1, 7):
                    acc = acc + wxs[h][j] * src[t, h, x + j]
                mid = src[t, h, x + PAD]
                p = mid - acc
                partial.append(p)
                start = mid if src is state0 else state0[t, h, x + PAD]
                new.append(start - acc - wys[h][3] * p)
            for d in (1, 2, 3):
                up = [pltpu.roll(p, LANES - d, 1) for p in partial]
                down = [pltpu.roll(p, d, 1) for p in partial]
                for h in range(halves):
                    u = up[h] if h == halves - 1 else jnp.where(lane < LANES - d, up[h], up[h + 1])
                    w = down[h] if h == 0 else jnp.where(lane >= d, down[h], down[h - 1])
                    new[h] = new[h] - (wys[h][3 + d] * u + wys[h][3 - d] * w)
            for h in range(halves):
                dst[t, h, x + off] = new[h]
            if sums is not None:
                net, pos = sums[2 * i], sums[2 * i + 1]
                for v in new:
                    net, pos = net + v, pos + jnp.maximum(v, 0.0)
                out += [net, pos]
        return tuple(out)

    stat[...] = jnp.zeros((SUB, LANES), jnp.float32)
    for s in range(3):
        for c in range(chunks):
            wait_halo(s, c)
            if s < 2:

                @pl.loop(0, deep)
                def _(x):
                    stage(c, states[s], states[s + 1], PAD, BETAS[s], x, None)

                start_halo(s + 1, c)
                continue
            z = jnp.zeros((SUB, LANES), jnp.float32)
            sums = lax.fori_loop(
                0, deep, lambda x, v: stage(c, states[s], result, 0, BETAS[s], x, v),
                (z,) * (2 * width))
            for lv in range(lev):
                deliver(result.at[tile_range(c), lv % halves, pl.ds((lv // halves) * rows, rows)],
                        back.at[my_lev, tile_range(c)], mate(lv),
                        out_send.at[lv, c], out_recv.at[my_lev, c])
            acc = stat[...]
            for i in range(width):
                t = c * width + i
                net = jnp.sum(sums[2 * i], axis=1, keepdims=True)
                pos = jnp.sum(sums[2 * i + 1], axis=1, keepdims=True)
                acc = jnp.where(lane == t, net, jnp.where(lane == tiles + t, pos, acc))
            stat[...] = acc

    def send_stat(k, carry):
        dev = (k + me) % n
        deliver(stat, stats.at[me], dev, s_send.at[dev], s_recv.at[me])
        return carry

    lax.fori_loop(0, n, send_stat, 0)

    sub = lax.broadcasted_iota(jnp.int32, (SUB, LANES), 0)
    for t in range(tiles):
        tile = jnp.zeros((SUB, LANES), jnp.float32)
        for i in range(SUB):
            if t * SUB + i < spec:
                tile = jnp.where(sub == i, rate_ref[t * SUB + i], tile)
        prate[pl.ds(t * SUB, SUB), :] = tile
    loads[2].wait()
    loads[3].wait()
    ks = [diff_ref[lv] for lv in range(lev - 1)]
    zero = jnp.zeros((rows, LANES), jnp.float32)
    lower = [zero] + ks
    upper = ks + [zero]
    prev = None
    for lv in range(lev):
        pivot = 1.0 + lower[lv] + upper[lv]
        if lv:
            pivot = pivot + lower[lv] * prev
        inv = 1.0 / pivot
        prev = -upper[lv] * inv
        coef[0, pl.ds(lv * rows, rows), :] = inv
        coef[1, pl.ds(lv * rows, rows), :] = lower[lv]
        coef[2, pl.ds(lv * rows, rows), :] = -prev

    def stat_in(k, carry):
        landed(stats.at[k], s_recv.at[k])
        return carry

    for c in range(chunks):
        for lv in range(lev):
            landed(back.at[lv, tile_range(c)], out_recv.at[lv, c])
    lax.fori_loop(0, n, stat_in, 0)
    total = stats[0]
    for k in range(1, n):
        total = total + stats[k]

    fades = [None] * rows
    for t in range(tiles):
        have = min(SUB, spec - t * SUB)
        if have <= 0:
            continue
        scale = jnp.broadcast_to(
            total[:, t:t + 1] / total[:, tiles + t:tiles + t + 1], (SUB, LANES))
        rate = prate[pl.ds(t * SUB, SUB), :]
        for r in range(rows):
            emis = emis_ref[pl.ds(t * SUB * rows + r, have, stride=rows), :]
            if have < SUB:
                emis = jnp.concatenate(
                    [emis, jnp.zeros((SUB - have, LANES), jnp.float32)], axis=0)
            value = []
            for lv in range(lev):
                right = jnp.maximum(back[lv, t, r], 0.0) * scale
                if lv == 0:
                    right = right + emis
                else:
                    right = right + coef[1, pl.ds(lv * rows + r, 1), :] * value[-1]
                value.append(right * coef[0, pl.ds(lv * rows + r, 1), :])
            mixed = [None] * lev
            mixed[lev - 1] = value[lev - 1]
            for lv in range(lev - 2, -1, -1):
                mixed[lv] = value[lv] + coef[2, pl.ds(lv * rows + r, 1), :] * mixed[lv + 1]
            if t == 0:
                fade = [None] * lev
                above = jnp.zeros((1, LANES), jnp.float32)
                for lv in range(lev - 1, -1, -1):
                    mine = mixed[lv][0:1, :]
                    fade[lv] = jnp.exp((-0.5 / lev) * (above + 0.5 * mine))
                    above = above + mine
                fades[r] = fade
            for lv in range(lev):
                val = mixed[lv] * jnp.exp(-(rate * fades[r][lv]))
                out_ref[pl.ds(t * SUB * stride + lv * rows + r, have, stride=stride), :] = val[0:have]

    def wind_sent(o, lv, dev, at):
        pl.when(dev != me)(lambda: sent(wsend.at[lv], w_send.at[o, lv]))

    for_winds(wind_sent)
    for lv in range(lev):

        @pl.when(lv != my_lev)
        def _():
            for c in range(chunks):
                sent(send.at[lv, tile_range(c)], in_send.at[lv, c])
                sent(result.at[tile_range(c), lv % halves, pl.ds((lv // halves) * rows, rows)],
                     out_send.at[lv, c])

    for s in range(3):
        for c in range(chunks):
            own = tile_range(c)
            pl.when(has_up)(lambda: sent(states[s].at[own, :, pl.ds(deep, PAD)], h_send.at[s, c, 0]))
            pl.when(has_down)(lambda: sent(states[s].at[own, :, pl.ds(PAD, PAD)], h_send.at[s, c, 1]))

    def stat_sent(k, carry):
        sent(stat, s_send.at[(k + me) % n])
        return carry

    lax.fori_loop(1, n, stat_sent, 0)


def per_device(gx_n, halves, conc, winds, diffusivity, emission, photo_rate):
    spec, lev, rows, lanes = conc.shape
    span = lev // halves
    assert span * halves == lev and gx_n % span == 0
    n = gx_n * halves
    real = -(-spec // SUB)
    chunks = CHUNKS
    width = -(-real // chunks)
    tiles = chunks * width
    deep = span * rows
    dims = (spec, lev, rows, halves, gx_n, span, tiles, chunks)
    f32 = jnp.float32
    hbm = pl.BlockSpec(memory_space=pl.ANY)
    dma = pltpu.SemaphoreType.DMA
    slots = (span + 2) * halves
    out = pl.pallas_call(
        functools.partial(kernel, dims),
        out_shape=jax.ShapeDtypeStruct((spec * lev * rows, lanes), f32),
        in_specs=[hbm] * 4 + [pl.BlockSpec(memory_space=pltpu.SMEM)],
        out_specs=pl.BlockSpec(memory_space=pltpu.VMEM),
        scratch_shapes=[
            pltpu.VMEM((spec * lev * rows, lanes), f32),
            pltpu.VMEM((2 * lev * rows, lanes), f32),
            pltpu.VMEM((lev - 1, rows, lanes), f32),
            pltpu.VMEM((spec * rows, lanes), f32),
            pltpu.VMEM((lev, tiles, rows, SUB, lanes), f32),
            pltpu.VMEM((tiles, halves, deep + 2 * PAD, SUB, lanes), f32),
            pltpu.VMEM((tiles, halves, deep + 2 * PAD, SUB, lanes), f32),
            pltpu.VMEM((tiles, halves, deep + 2 * PAD, SUB, lanes), f32),
            pltpu.VMEM((tiles, halves, deep, SUB, lanes), f32),
            pltpu.VMEM((lev, tiles, rows, SUB, lanes), f32),
            pltpu.VMEM((lev, 2 * rows, lanes), f32),
            pltpu.VMEM((slots, 2 * rows, lanes), f32),
            pltpu.VMEM((2, halves, deep + 2 * SUB, lanes), f32),
            pltpu.VMEM((7, halves, deep, lanes), f32),
            pltpu.VMEM((7, halves, deep, lanes), f32),
            pltpu.VMEM((SUB, lanes), f32),
            pltpu.VMEM((n, SUB, lanes), f32),
            pltpu.VMEM((tiles * SUB, lanes), f32),
            pltpu.VMEM((3, lev * rows, lanes), f32),
            dma((4,)),
            dma((lev, chunks)), dma((lev, chunks)),
            dma((3, lev)), dma((slots,)),
            dma((3, chunks, 2)), dma((3, chunks, 2)),
            dma((lev, chunks)), dma((lev, chunks)),
            dma((n,)), dma((n,)),
        ],
        compiler_params=pltpu.CompilerParams(collective_id=0, has_side_effects=True),
    )(
        conc.reshape(spec * lev * rows, lanes),
        winds.reshape(2 * lev * rows, lanes),
        diffusivity,
        emission.reshape(spec * rows, lanes),
        photo_rate,
    )
    return out.reshape(spec, lev, rows, lanes)


def solution(mesh):
    halves = mesh.shape["gy"]
    gx_n = mesh.shape["gx"]
    return jax.shard_map(
        functools.partial(per_device, gx_n, halves),
        mesh=mesh,
        in_specs=(
            P(None, None, ("member", "gx"), "gy"),
            P(None, None, ("member", "gx"), "gy"),
            P(None, ("member", "gx"), "gy"),
            P(None, ("member", "gx"), "gy"),
            P(),
        ),
        out_specs=P(None, None, ("member", "gx"), "gy"),
        check_vma=False,
    )
```

profile of v0, /device:TPU:0, one launch (start us, length us, event | category | flops | bytes accessed | tf_op | source)
XLA Modules:
  0.0 39.3 jit_solution(9890155239227929760)
XLA Ops:
  0.0 37.4 %shard_map.55 = f32[1056,128]{1,0:T(8,128)} custom-call(f32[1056,128]{1,0:T(8,128)} %bitcast.5, f32[32,128]{1,0:T(8,128)} %bitcast.7, f32[3,4,128]{2,1,0:T(4,128)} %diff_hbm.1, f32[264,128]{1,0:T(8,128)} %bitcast.6, f32[66]{0:T(128)} %rate_ref.1), custom_call_target="tpu_custom_call" | custom-call | tf_op jit(solution)/shard_map/pallas_call | solution.py:396
  37.5 1.9 %copy.7 = f32[66,4,4,128]{3,2,1,0:T(4,128)} copy(f32[66,4,4,128]{3,2,1,0:T(4,128)} %bitcast.4) | data formatting | bytes 1081344
where the time goes:
time: 39.6 us; the launch traced here: 39.3 us
  Pallas kernels  37.4 us (94%)
  local copies, waits for them, and re-layouts  1.88 us (5%)
    pallas_call x1, Pallas kernels, per_device(): pl.pallas_call(functools.partial(kernel, dims), out_shape=jax.ShapeDtypeS...  37.4 us
    unnamed x1, local copies, waits for them, and re-layouts  1.88 us

commit v1 on v0

--- a/solution.py
+++ b/solution.py
@@ -31,12 +31,12 @@
     return [-m[0]] + [p[j] - m[j + 1] for j in range(5)] + [p[5]]
 
 
-def kernel(dims, conc_hbm, wind_hbm, diff_hbm, emis_hbm, rate_ref, out_ref,
+def kernel(dims, conc_hbm, wind_hbm, diff_hbm, emis_hbm, rate_ref, out_hbm,
            conc_ref, wind_ref, diff_ref, emis_ref,
            send, state0, state_a, state_b, result, back, wsend, wrecv, cbuf, wx, wy,
            stat, stats, prate, coef,
            load_sem, in_send, in_recv, w_send, w_recv, h_send, h_recv,
-           out_send, out_recv, s_send, s_recv):
+           out_send, out_recv, s_send, s_recv, out_ref, store_sem):
     spec, lev, rows, halves, gx_n, span, tiles, chunks = dims
     n = gx_n * halves
     width = tiles // chunks
@@ -316,6 +316,7 @@
         total = total + stats[k]
 
     fades = [None] * rows
+    stores = []
     for t in range(tiles):
         have = min(SUB, spec - t * SUB)
         if have <= 0:
@@ -351,6 +352,9 @@
             for lv in range(lev):
                 val = mixed[lv] * jnp.exp(-(rate * fades[r][lv]))
                 out_ref[pl.ds(t * SUB * stride + lv * rows + r, have, stride=stride), :] = val[0:have]
+        done = pl.ds(t * SUB * stride, have * stride)
+        stores.append(pltpu.make_async_copy(out_ref.at[done], out_hbm.at[done], store_sem.at[t]))
+        stores[-1].start()
 
     def wind_sent(o, lv, dev, at):
         pl.when(dev != me)(lambda: sent(wsend.at[lv], w_send.at[o, lv]))
@@ -376,6 +380,8 @@
         return carry
 
     lax.fori_loop(1, n, stat_sent, 0)
+    for store in stores:
+        store.wait()
 
 
 def per_device(gx_n, halves, conc, winds, diffusivity, emission, photo_rate):
@@ -397,7 +403,7 @@
         functools.partial(kernel, dims),
         out_shape=jax.ShapeDtypeStruct((spec * lev * rows, lanes), f32),
         in_specs=[hbm] * 4 + [pl.BlockSpec(memory_space=pltpu.SMEM)],
-        out_specs=pl.BlockSpec(memory_space=pltpu.VMEM),
+        out_specs=hbm,
         scratch_shapes=[
             pltpu.VMEM((spec * lev * rows, lanes), f32),
             pltpu.VMEM((2 * lev * rows, lanes), f32),
@@ -424,6 +430,7 @@
             dma((3, chunks, 2)), dma((3, chunks, 2)),
             dma((lev, chunks)), dma((lev, chunks)),
             dma((n,)), dma((n,)),
+            pltpu.VMEM((spec * lev * rows, lanes), f32), dma((tiles,)),
         ],
         compiler_params=pltpu.CompilerParams(collective_id=0, has_side_effects=True),
     )(

time: 39.6 us -> 39.2 us (0.990)
  no operation moved by 1% of the time
where the time goes in v1:
time: 39.2 us; the launch traced here: 39 us
  Pallas kernels  37.1 us (95%)
  local copies, waits for them, and re-layouts  1.88 us (5%)
    pallas_call x1, Pallas kernels, per_device(): pl.pallas_call(functools.partial(kernel, dims), out_shape=jax.ShapeDtypeS...  37.1 us
    unnamed x1, local copies, waits for them, and re-layouts  1.88 us

profile of v1, /device:TPU:0, one launch (start us, length us, event | category | flops | bytes accessed | tf_op | source)
XLA Modules:
  0.0 39.0 jit_solution(69321582885787999)
XLA Ops:
  0.0 37.1 %shard_map.55 = f32[1056,128]{1,0:T(8,128)} custom-call(f32[1056,128]{1,0:T(8,128)} %bitcast.5, f32[32,128]{1,0:T(8,128)} %bitcast.7, f32[3,4,128]{2,1,0:T(4,128)} %diff_hbm.1, f32[264,128]{1,0:T(8,128)} %bitcast.6, f32[66]{0:T(128)} %rate_ref.1), custom_call_target="tpu_custom_call" | custom-call | tf_op jit(solution)/shard_map/pallas_call | solution.py:402
  37.1 1.9 %copy.7 = f32[66,4,4,128]{3,2,1,0:T(4,128)} copy(f32[66,4,4,128]{3,2,1,0:T(4,128)} %bitcast.4) | data formatting | bytes 1081344
